TPU v7x, 32 devices: a whole 2x2x4 slice. The times are simulated.
32 devices in a mesh: blk: 2 (over x), wide: 16 (over z, y, core).
Axes of the slice: x: 2, y: 2, z: 4, core: 2. Of those that a mesh axis runs over, the one named last changes fastest.
Arguments:
- volume: float32 [2, 2, 512, 896], P('blk', None, 'wide'), may hold values from -1.6 to 1.6
- path_lengths: float32 [2, 2, 2], replicated, may hold values from 0.5 to 2
- probe: float32 [2, 128, 128], replicated, may hold values from -6 to 6
- measured: bfloat16 [2, 16, 14, 128, 128], P('blk', 'wide'), may hold values from 0.19921875 to 3
- jitter: int32 [2, 2, 16, 14], P(None, 'blk', 'wide'), may hold values from 0 to 15
- step_sizes: float32 [2], replicated, may hold values from 0.02 to 0.2
Outputs:
- new_volume: float32 [2, 2, 512, 896], P('blk', None, 'wide')
- misfit: float32 [], replicated
All inputs are finite; a program needn't handle non-finite values.
Results may differ from a plain program's by a relative error of at most 0.0003.
Values sent between devices are 32-bit elements; how exact they have to be, the bound alone decides.
A program may use at most 64 MiB of HBM per device.

v0:
```python
import math
import jax
import jax.numpy as jnp
from jax import lax
from jax.sharding import PartitionSpec as P

ROWS_DEV = 32
PATCH = 128
CSTEP = 64
highest = lax.Precision.HIGHEST
floor_value = 0.25


def passed_along(value, axis, steps):
    count = lax.axis_size(axis)
    pairs = [(source, (source + steps) % count) for source in range(count)]
    return lax.ppermute(value, axis, pairs)


def from_behind(shard, axis, by):
    count = lax.axis_size(axis)
    pairs = [(i, i + by) for i in range(count) if 0 <= i + by < count]
    return lax.ppermute(shard, axis, pairs)


def dft_tables(length):
    grid = jnp.arange(length, dtype=jnp.int32)
    product = grid[:, None] * grid[None, :] % length
    angles = product.astype(jnp.float32) * (2.0 * math.pi / length)
    factor = 1.0 / math.sqrt(length)
    return (jnp.cos(angles) * factor, -jnp.sin(angles) * factor)


def left_apply(table, batch):
    return jnp.einsum("jk,bkl->bjl", table, batch, precision=highest)


def right_apply(batch, table):
    return jnp.einsum("bjk,kl->bjl", batch, table, precision=highest)


def transform(real_in, imag_in, cos_table, sin_table):
    mid_real = left_apply(cos_table, real_in) - left_apply(sin_table, imag_in)
    mid_imag = left_apply(cos_table, imag_in) + left_apply(sin_table, real_in)
    out_real = right_apply(mid_real, cos_table) - right_apply(mid_imag, sin_table)
    out_imag = right_apply(mid_real, sin_table) + right_apply(mid_imag, cos_table)
    return (out_real, out_imag)


def strip_update(
    strip_real,
    strip_imaginary,
    probe,
    measured,
    jitter_rows,
    jitter_cols,
    row_corner,
    column_corner,
):
    patch_len = probe.shape[-1]
    number = measured.shape[0]
    cos_table, sin_table = dft_tables(patch_len)
    starts_row = row_corner + jitter_rows
    starts_col = column_corner + CSTEP * jnp.arange(number, dtype=jnp.int32) + jitter_cols

    def window(image, top, left):
        return lax.dynamic_slice(image, (top, left), (patch_len, patch_len))

    pick = jax.vmap(window, in_axes=(None, 0, 0))
    obj_real = pick(strip_real, starts_row, starts_col)
    obj_imag = pick(strip_imaginary, starts_row, starts_col)
    probe_real = probe[0]
    probe_imag = probe[1]
    wave_real = probe_real * obj_real - probe_imag * obj_imag
    wave_imag = probe_real * obj_imag + probe_imag * obj_real
    far_real, far_imag = transform(wave_real, wave_imag, cos_table, sin_table)
    modulus = jnp.sqrt(far_real * far_real + far_imag * far_imag)
    target = measured.astype(jnp.float32)
    error = modulus - target
    partial_misfit = jnp.sum(error * error)
    ratio = target / jnp.maximum(modulus, floor_value)
    back_real, back_imag = transform(ratio * far_real, ratio * far_imag, cos_table, -sin_table)
    diff_real = back_real - wave_real
    diff_imag = back_imag - wave_imag
    corr_real = probe_real * diff_real + probe_imag * diff_imag
    corr_imag = probe_real * diff_imag - probe_imag * diff_real

    def place(position, sums):
        acc_real, acc_imag = sums
        top = starts_row[position]
        left = starts_col[position]
        acc_real = lax.dynamic_update_slice(
            acc_real, window(acc_real, top, left) + corr_real[position], (top, left)
        )
        acc_imag = lax.dynamic_update_slice(
            acc_imag, window(acc_imag, top, left) + corr_imag[position], (top, left)
        )
        return (acc_real, acc_imag)

    zeros = jnp.zeros(strip_real.shape, strip_real.dtype)
    acc_real, acc_imag = lax.fori_loop(0, number, place, (zeros, zeros))
    return (acc_real, acc_imag, partial_misfit)


def body(volume, path_lengths, probe, measured, jitter, step_sizes):
    group = lax.axis_index("blk")
    groups = lax.axis_size("blk")
    column = lax.axis_index("wide")
    columns = lax.axis_size("wide")
    slab = volume[0]
    row_len = slab.shape[1]
    col_len = slab.shape[2]
    margin = probe.shape[-1] // 2
    own_paths = lax.dynamic_index_in_dim(path_lengths, group, 1, keepdims=False)

    def slab_term(angle, weight):
        coeffs = lax.dynamic_index_in_dim(own_paths, angle, 0, keepdims=False) * weight
        return jnp.einsum("l,lrc->rc", coeffs, slab, precision=highest)

    def cycle_step(section, carried):
        carried = passed_along(carried, "blk", 1)
        angle = (group - section) % groups
        weight = jnp.where(section < groups, 1.0, 0.0).astype(jnp.float32)
        return carried + slab_term(angle, weight)

    projection = lax.fori_loop(
        1, groups + 1, cycle_step, slab_term(group, jnp.ones((), jnp.float32))
    )
    sources = (2, 1, 0, -1, -2)
    pieces_real = []
    pieces_imag = []
    for offset in sources:
        if offset == 0:
            got_phase = projection
        else:
            got_phase = from_behind(projection, "wide", offset)
        source = column - offset
        valid = ((source >= 0) & (source < columns)).astype(jnp.float32)
        pieces_real.append(jnp.cos(got_phase) * valid)
        pieces_imag.append(jnp.sin(got_phase) * valid)
    ext_real = jnp.concatenate(pieces_real, 0)
    ext_imag = jnp.concatenate(pieces_imag, 0)
    strip_real = jnp.pad(ext_real, ((0, 0), (margin, margin)))
    strip_imaginary = jnp.pad(ext_imag, ((0, 0), (margin, margin)))
    row_corner = ROWS_DEV // 4
    column_corner = PATCH // 4 - ROWS_DEV // 4
    acc_real, acc_imag, local_misfit = strip_update(
        strip_real,
        strip_imaginary,
        probe,
        measured[0, 0],
        jitter[0, 0, 0],
        jitter[1, 0, 0],
        row_corner,
        column_corner,
    )
    acc_real = acc_real[:, margin : margin + col_len]
    acc_imag = acc_imag[:, margin : margin + col_len]

    def rows_of(array, slot):
        return array[slot * row_len : (slot + 1) * row_len]

    total_real = rows_of(acc_real, 2)
    total_imag = rows_of(acc_imag, 2)
    for offset in (-2, -1, 1, 2):
        got_real, got_imag = from_behind(
            (rows_of(acc_real, 2 + offset), rows_of(acc_imag, 2 + offset)), "wide", offset
        )
        total_real = total_real + got_real
        total_imag = total_imag + got_imag
    gradient = rows_of(ext_real, 2) * total_imag - rows_of(ext_imag, 2) * total_real
    total_misfit = lax.psum(local_misfit, ("blk", "wide"))
    scaled = step_sizes[:, None] * own_paths
    coeffs = scaled
    update = jnp.einsum(
        "al,arc->lrc",
        coeffs,
        lax.all_gather(gradient[None], "blk", axis=0, tiled=True),
        precision=highest,
    )
    return ((slab - update)[None], total_misfit)


def solution(mesh):
    in_specs = (
        P("blk", None, "wide", None),
        P(),
        P(),
        P("blk", "wide", None, None, None),
        P(None, "blk", "wide", None),
        P(),
    )
    out_specs = (P("blk", None, "wide", None), P())
    return jax.shard_map(body, mesh=mesh, in_specs=in_specs, out_specs=out_specs, check_vma=False)
```

profile of v0, /device:TPU:0, one launch (start us, length us, event | category | flops | bytes accessed | tf_op | source)
XLA Modules:
  0.0 310.6 jit_solution(9081547119739849727)
XLA Ops:
  3.4 11.1 %while.32 = (s32[]{:T(128)}, f32[32,896]{1,0:T(8,128)S(1)}, s32[]{:T(128)}, f32[2,2]{1,0:T(2,128)S(1)}, f32[2,32,896]{2,1,0:T(8,128)S(1)}, /*index=5*/s32[]{:T(128)}, s32[]{:T(128)}, s32[]{:T(128)}, f32[]{:T(128)}, f32[]{:T(128)}) while((s32[]{:T(128)}, f32[32,896]{1,0:T(8,128)S(1)}, s32[]{:T(128)}, f32[2,2]{1,0:T(2,128)S(1)}, ...), condition=%wide.region_1.2_spmd, body=%wide.region_0.1_spmd.sunk | while | flops 716821 | bytes 1147718 | solution.py:126
  3.4 3.0 collective-permute-start
  7.4 2.2 collective-permute-done
  9.6 1.8 collective-permute-start
  12.4 2.1 collective-permute-done
  14.5 3.7 %collective-permute-start.1 = (f32[32,896]{1,0:T(8,128)S(1)}, f32[32,896]{1,0:T(8,128)S(1)}, u32[]{:S(2)}, u32[]{:S(2)}) collective-permute-start(f32[32,896]{1,0:T(8,128)S(1)} %get-tuple-element.260), channel_id=1, source_target_pairs={{0,2},{1,3},{2,4},{3,5},{4,6},{5,7},{6,8},{7,9},{8,10},{9,11},{10,... | collective-permute-start | bytes 344072 | tf_op jit(solution)/shard_map/ppermute | solution.py:23
  24.9 5.7 %collective-permute-done.4 = f32[32,896]{1,0:T(8,128)S(1)} collective-permute-done((f32[32,896]{1,0:T(8,128)S(1)}, f32[32,896]{1,0:T(8,128)S(1)}, u32[]{:S(2)}, u32[]{:S(2)}) %collective-permute-start.4) | collective-permute-done | bytes 114720 | tf_op jit(solution)/shard_map/ppermute | solution.py:23
  31.4 28.7 %while.34 = (s32[]{:T(128)}, f32[160,1024]{1,0:T(8,128)S(1)}, s32[14,2]{0,1:T(2,128)S(1)}, f32[14,128,128]{2,1,0:T(8,128)S(1)}, s32[]{:T(128)}) while((s32[]{:T(128)}, f32[160,1024]{1,0:T(8,128)S(1)}, s32[14,2]{0,1:T(2,128)S(1)}, f32[14,128,128]{2,1,0:T(8,128)S(1)}, s32[]{:T(128)}) %tuple.120), condition=%wide.while_cond, body=%wide.while_body.sunk | while | flops 2 | bytes 131181 | solution.py:67
  60.3 27.1 %while.35 = (s32[]{:T(128)}, f32[160,1024]{1,0:T(8,128)S(1)}, s32[14,2]{0,1:T(2,128)S(1)}, f32[14,128,128]{2,1,0:T(8,128)S(1)}, s32[]{:T(128)}) while((s32[]{:T(128)}, f32[160,1024]{1,0:T(8,128)S(1)}, s32[14,2]{0,1:T(2,128)S(1)}, f32[14,128,128]{2,1,0:T(8,128)S(1)}, s32[]{:T(128)}) %tuple.127), condition=%wide.while_cond.1, body=%wide.while_body.1.sunk | while | flops 2 | bytes 131181 | solution.py:67
  87.7 1.7 fusion.42
  89.5 1.7 fusion.46
  91.2 1.8 fusion.10
  93.0 1.7 fusion.44
  94.7 1.7 fusion.31
  96.4 1.8 fusion.9
  98.2 1.9 convolution_subtract_fusion.2
  100.2 2.6 fusion.13
  102.8 2.2 fusion.14
  105.0 2.2 fusion.18
  107.1 2.2 fusion.8
  109.3 1.8 fusion.26
  111.1 1.9 fusion.38
  113.1 2.2 fusion.7
  115.3 1.8 fusion.5
  117.0 1.9 multiply_subtract_fusion
  119.1 118.2 %while.33 = (s32[]{:T(128)}, f32[160,1024]{1,0:T(8,128)S(1)}, f32[160,1024]{1,0:T(8,128)S(1)}, s32[14]{0:T(128)S(1)}, s32[14]{0:T(128)S(1)}, /*index=5*/f32[14,1...) while((s32[]{:T(128)}, f32[160,1024]{1,0:T(8,128)S(1)}, ...), condition=%wide.region_3.4_spmd, body=%wide.region_2.3_spmd.sunk | while | flops 32776 | bytes 655581 | solution.py:101
  124.1 1.7 dynamic_update_slice.17
  125.8 1.7 dynamic_update_slice.16
  132.5 1.7 dynamic_update_slice.17
  134.2 1.7 dynamic_update_slice.16
  149.4 1.7 dynamic_update_slice.17
  151.1 1.7 dynamic_update_slice.16
  166.3 1.7 dynamic_update_slice.17
  168.0 1.7 dynamic_update_slice.16
  174.7 1.7 dynamic_update_slice.17
  183.1 1.7 dynamic_update_slice.17
  184.9 1.7 dynamic_update_slice.16
  191.6 1.7 dynamic_update_slice.17
  193.3 1.7 dynamic_update_slice.16
  208.5 1.7 dynamic_update_slice.17
  233.8 1.7 dynamic_update_slice.17
  235.6 1.7 dynamic_update_slice.16
  238.8 3.0 collective-permute-start.11
  241.8 4.5 %collective-permute-start.12 = (f32[32,896]{1,0:T(8,128)S(1)}, f32[32,896]{1,0:T(8,128)S(1)}, u32[]{:S(2)}, u32[]{:S(2)}) collective-permute-start(f32[32,896]{1,0:T(8,128)S(1)} %get-tuple-element.348), channel_id=1, source_target_pairs={{0,2},{1,3},{2,4},{3,5},{4,6},{5,7},{6,8},{7,9},{8,10},{9,11},{10,... | collective-permute-start | bytes 344072 | tf_op jit(solution)/shard_map/ppermute | solution.py:23
  249.2 3.5 %collective-permute-start.7 = (f32[32,896]{1,0:T(8,128)S(1)}, f32[32,896]{1,0:T(8,128)S(1)}, u32[]{:S(2)}, u32[]{:S(2)}) collective-permute-start(f32[32,896]{1,0:T(8,128)S(1)} %get-tuple-element.345), channel_id=1, source_target_pairs={{0,1},{1,2},{2,3},{3,4},{4,5},{5,6},{6,7},{7,8},{8,9},{9,10},{10,1... | collective-permute-start | bytes 344072 | tf_op jit(solution)/shard_map/ppermute | solution.py:23
  252.7 4.3 %collective-permute-start.8 = (f32[32,896]{1,0:T(8,128)S(1)}, f32[32,896]{1,0:T(8,128)S(1)}, u32[]{:S(2)}, u32[]{:S(2)}) collective-permute-start(f32[32,896]{1,0:T(8,128)S(1)} %get-tuple-element.344), channel_id=1, source_target_pairs={{0,2},{1,3},{2,4},{3,5},{4,6},{5,7},{6,8},{7,9},{8,10},{9,11},{10,... | collective-permute-start | bytes 344072 | tf_op jit(solution)/shard_map/ppermute | solution.py:23
  258.3 43.2 %psum.7 = f32[]{:T(128)} all-reduce(f32[]{:T(128)} %get-tuple-element.365), channel_id=1, replica_groups=mesh['blk'=2,'wide'=16] {'blk','wide'}, use_global_device_ids=true, to_apply=%region_5.6 | all-reduce | flops 1 | bytes 8 | tf_op jit(solution)/shard_map/psum | solution.py:172
  302.0 5.8 %all-gather = f32[64,896]{1,0:T(8,128)S(1)} all-gather(f32[32,896]{1,0:T(8,128)S(1)} %multiply_subtract_fusion.2), channel_id=2, replica_groups=mesh['blk'=2,'wide'=16] {'blk'}, dimensions={0}, use_global_device_ids=true | all-gather | bytes 344064 | tf_op jit(solution)/shard_map/all_gather | solution.py:178
  (201 shorter events, 115.2 us)
Async XLA Ops:
  0.6 1.2 copy-start
  1.8 0.7 copy-start.1
  3.4 18.8 %copy-start.4 = (f32[2,128,128]{2,1,0:T(8,128)S(1)}, f32[2,128,128]{2,1,0:T(8,128)}, u32[]{:S(2)}) copy-start(f32[2,128,128]{2,1,0:T(8,128)} %param.12) | copy-start | bytes 393220
  3.4 6.2 %collective-permute-start = (f32[32,896]{1,0:T(8,128)S(1)}, f32[32,896]{1,0:T(8,128)S(1)}, u32[]{:S(2)}, u32[]{:S(2)}) collective-permute-start(f32[32,896]{1,0:T(8,128)S(1)} %get-tuple-element.514), channel_id=1, source_target_pairs={{0,16},{16,0},{1,17},{17,1},{2,18},{18,2},{3,19},{19,3},{4,20},{20... | collective-permute-start | bytes 344072 | tf_op jit(solution)/shard_map/while/body/eval_jaxpr/ppermute | solution.py:17
  9.6 4.9 %collective-permute-start = (f32[32,896]{1,0:T(8,128)S(1)}, f32[32,896]{1,0:T(8,128)S(1)}, u32[]{:S(2)}, u32[]{:S(2)}) collective-permute-start(f32[32,896]{1,0:T(8,128)S(1)} %get-tuple-element.514), channel_id=1, source_target_pairs={{0,16},{16,0},{1,17},{17,1},{2,18},{18,2},{3,19},{19,3},{4,20},{20... | collective-permute-start | bytes 344072 | tf_op jit(solution)/shard_map/while/body/eval_jaxpr/ppermute | solution.py:17
  14.5 7.6 %copy-start.5 = (s32[2,1,1,14]{3,2,1,0:T(1,128)S(1)}, s32[2,1,1,14]{3,2,1,0:T(1,128)}, u32[]{:S(2)}) copy-start(s32[2,1,1,14]{3,2,1,0:T(1,128)} %param.14) | copy-start | bytes 340
  14.5 7.7 %collective-permute-start.1 = (f32[32,896]{1,0:T(8,128)S(1)}, f32[32,896]{1,0:T(8,128)S(1)}, u32[]{:S(2)}, u32[]{:S(2)}) collective-permute-start(f32[32,896]{1,0:T(8,128)S(1)} %get-tuple-element.260), channel_id=1, source_target_pairs={{0,2},{1,3},{2,4},{3,5},{4,6},{5,7},{6,8},{7,9},{8,10},{9,11},{10,... | collective-permute-start | bytes 344072 | tf_op jit(solution)/shard_map/ppermute | solution.py:23
  18.2 4.5 %collective-permute-start.2 = (f32[32,896]{1,0:T(8,128)S(1)}, f32[32,896]{1,0:T(8,128)S(1)}, u32[]{:S(2)}, u32[]{:S(2)}) collective-permute-start(f32[32,896]{1,0:T(8,128)S(1)} %get-tuple-element.260), channel_id=1, source_target_pairs={{0,1},{1,2},{2,3},{3,4},{4,5},{5,6},{6,7},{7,8},{8,9},{9,10},{10,1... | collective-permute-start | bytes 344072 | tf_op jit(solution)/shard_map/ppermute | solution.py:23
  19.5 5.0 %collective-permute-start.3 = (f32[32,896]{1,0:T(8,128)S(1)}, f32[32,896]{1,0:T(8,128)S(1)}, u32[]{:S(2)}, u32[]{:S(2)}) collective-permute-start(f32[32,896]{1,0:T(8,128)S(1)} %get-tuple-element.260), channel_id=1, source_target_pairs={{1,0},{2,1},{3,2},{4,3},{5,4},{6,5},{7,6},{8,7},{9,8},{10,9},{11,1... | collective-permute-start | bytes 344072 | tf_op jit(solution)/shard_map/ppermute | solution.py:23
  20.8 9.8 %collective-permute-start.4 = (f32[32,896]{1,0:T(8,128)S(1)}, f32[32,896]{1,0:T(8,128)S(1)}, u32[]{:S(2)}, u32[]{:S(2)}) collective-permute-start(f32[32,896]{1,0:T(8,128)S(1)} %get-tuple-element.260), channel_id=1, source_target_pairs={{2,0},{3,1},{4,2},{5,3},{6,4},{7,5},{8,6},{9,7},{10,8},{11,9},{12,... | collective-permute-start | bytes 344072 | tf_op jit(solution)/shard_map/ppermute | solution.py:23
  98.2 1.9 copy-start.3
  237.5 11.7 %collective-permute-start.10 = (f32[32,896]{1,0:T(8,128)S(1)}, f32[32,896]{1,0:T(8,128)S(1)}, u32[]{:S(2)}, u32[]{:S(2)}) collective-permute-start(f32[32,896]{1,0:T(8,128)S(1)} %get-tuple-element.350), channel_id=1, source_target_pairs={{1,0},{2,1},{3,2},{4,3},{5,4},{6,5},{7,6},{8,7},{9,8},{10,9},{11,1... | collective-permute-start | bytes 344072 | tf_op jit(solution)/shard_map/ppermute | solution.py:23
  238.8 13.9 %collective-permute-start.11 = (f32[32,896]{1,0:T(8,128)S(1)}, f32[32,896]{1,0:T(8,128)S(1)}, u32[]{:S(2)}, u32[]{:S(2)}) collective-permute-start(f32[32,896]{1,0:T(8,128)S(1)} %get-tuple-element.349), channel_id=1, source_target_pairs={{0,1},{1,2},{2,3},{3,4},{4,5},{5,6},{6,7},{7,8},{8,9},{9,10},{10,1... | collective-permute-start | bytes 344072 | tf_op jit(solution)/shard_map/ppermute | solution.py:23
  241.8 15.1 %collective-permute-start.12 = (f32[32,896]{1,0:T(8,128)S(1)}, f32[32,896]{1,0:T(8,128)S(1)}, u32[]{:S(2)}, u32[]{:S(2)}) collective-permute-start(f32[32,896]{1,0:T(8,128)S(1)} %get-tuple-element.348), channel_id=1, source_target_pairs={{0,2},{1,3},{2,4},{3,5},{4,6},{5,7},{6,8},{7,9},{8,10},{9,11},{10,... | collective-permute-start | bytes 344072 | tf_op jit(solution)/shard_map/ppermute | solution.py:23
  246.6 54.9 %collective-permute-start.5 = (f32[32,896]{1,0:T(8,128)S(1)}, f32[32,896]{1,0:T(8,128)S(1)}, u32[]{:S(2)}, u32[]{:S(2)}) collective-permute-start(f32[32,896]{1,0:T(8,128)S(1)} %get-tuple-element.343), channel_id=1, source_target_pairs={{2,0},{3,1},{4,2},{5,3},{6,4},{7,5},{8,6},{9,7},{10,8},{11,9},{12,... | collective-permute-start | bytes 344072 | tf_op jit(solution)/shard_map/ppermute | solution.py:23
  247.9 53.6 %collective-permute-start.6 = (f32[32,896]{1,0:T(8,128)S(1)}, f32[32,896]{1,0:T(8,128)S(1)}, u32[]{:S(2)}, u32[]{:S(2)}) collective-permute-start(f32[32,896]{1,0:T(8,128)S(1)} %get-tuple-element.346), channel_id=1, source_target_pairs={{1,0},{2,1},{3,2},{4,3},{5,4},{6,5},{7,6},{8,7},{9,8},{10,9},{11,1... | collective-permute-start | bytes 344072 | tf_op jit(solution)/shard_map/ppermute | solution.py:23
  249.2 52.3 %collective-permute-start.7 = (f32[32,896]{1,0:T(8,128)S(1)}, f32[32,896]{1,0:T(8,128)S(1)}, u32[]{:S(2)}, u32[]{:S(2)}) collective-permute-start(f32[32,896]{1,0:T(8,128)S(1)} %get-tuple-element.345), channel_id=1, source_target_pairs={{0,1},{1,2},{2,3},{3,4},{4,5},{5,6},{6,7},{7,8},{8,9},{9,10},{10,1... | collective-permute-start | bytes 344072 | tf_op jit(solution)/shard_map/ppermute | solution.py:23
  252.7 48.8 %collective-permute-start.8 = (f32[32,896]{1,0:T(8,128)S(1)}, f32[32,896]{1,0:T(8,128)S(1)}, u32[]{:S(2)}, u32[]{:S(2)}) collective-permute-start(f32[32,896]{1,0:T(8,128)S(1)} %get-tuple-element.344), channel_id=1, source_target_pairs={{0,2},{1,3},{2,4},{3,5},{4,6},{5,7},{6,8},{7,9},{8,10},{9,11},{10,... | collective-permute-start | bytes 344072 | tf_op jit(solution)/shard_map/ppermute | solution.py:23
  257.0 44.5 %collective-permute-start.9 = (f32[32,896]{1,0:T(8,128)S(1)}, f32[32,896]{1,0:T(8,128)S(1)}, u32[]{:S(2)}, u32[]{:S(2)}) collective-permute-start(f32[32,896]{1,0:T(8,128)S(1)} %get-tuple-element.347), channel_id=1, source_target_pairs={{2,0},{3,1},{4,2},{5,3},{6,4},{7,5},{8,6},{9,7},{10,8},{11,9},{12,... | collective-permute-start | bytes 344072 | tf_op jit(solution)/shard_map/ppermute | solution.py:23
  301.9 5.9 %copy-start.2 = (f32[1,2,32,896]{3,1,2,0:T(2,128)S(1)}, f32[1,2,32,896]{3,1,2,0:T(2,128)}, u32[]{:S(2)}) copy-start(f32[1,2,32,896]{3,1,2,0:T(2,128)} %copy-done.1) | copy-start | bytes 688132
  307.8 0.7 copy-start.6
where the time goes:
time: 317 us; the launch traced here: 311 us
  local copies, waits for them, and re-layouts  124 us (39%)
  loops' own time  52.8 us (17%)
  blocking collectives  49 us (15%)
  matrix products  35.1 us (11%)
  starting transfers between devices  32.9 us (10%)
  waiting for transfers between devices  11 us (3%)
  other arithmetic  4.47 us (1%)
    gather x84, local copies, waits for them, and re-layouts  54.7 us
    another operation x1, loops' own time, strip_update(): acc_real, acc_imag = lax.fori_loop(0, number, place, (zeros, zeros))  51.7 us
    psum x1, blocking collectives, body(): total_misfit = lax.psum(local_misfit, ('blk', 'wide'))  43.2 us
    ppermute x12, starting transfers between devices, from_behind(): return lax.ppermute(shard, axis, pairs)  28.1 us
    dynamic_update_slice x14, local copies, waits for them, and re-layouts, place(): lax.dynamic_update_slice(acc_imag, window(acc_imag, top, left) + corr_ima...  23.8 us
    dynamic_update_slice x14, local copies, waits for them, and re-layouts, place(): lax.dynamic_update_slice(acc_real, window(acc_real, top, left) + corr_rea...  23.8 us
    dot_general x8, matrix products, left_apply(): return jnp.einsum('jk,bkl->bjl', table, batch, precision=highest)  15.7 us
    dot_general x8, matrix products, right_apply(): return jnp.einsum('bjk,kl->bjl', batch, table, precision=highest)  15.4 us
  transfers between devices with their start and end apart: 14, of which 4 were waited for; matrix products, arithmetic and copies ran while one was open for 1% of the time, Pallas kernels for 0%

commit v1 on v0

--- a/solution.py
+++ b/solution.py
@@ -169,7 +169,7 @@
         total_real = total_real + got_real
         total_imag = total_imag + got_imag
     gradient = rows_of(ext_real, 2) * total_imag - rows_of(ext_imag, 2) * total_real
-    total_misfit = lax.psum(local_misfit, ("blk", "wide"))
+    total_misfit = jnp.sum(lax.all_gather(local_misfit, ("blk", "wide")), axis=0)
     scaled = step_sizes[:, None] * own_paths
     coeffs = scaled
     update = jnp.einsum(

time: 317 us -> 329 us (1.038)
  loops' own time: 52.8 us -> 59.8 us
  local copies, waits for them, and re-layouts: 124 us -> 129 us
    psum x1 -> x0, blocking collectives: 43.2 us -> none  [body(): total_misfit = lax.psum(local_misfit, ('blk', 'wide'))]
    unnamed x0 -> x1, blocking collectives: none -> 42.9 us
    another operation x1, loops' own time: 51.7 us -> 58.7 us  [strip_update(): acc_real, acc_imag = lax.fori_loop(0, number, place, (zeros, zeros))]
  transfers between devices with their start and end apart: 14 -> 14, of which waited for: 4 -> 4; matrix products, arithmetic and copies ran while one was open for 1% -> 2% of each run, Pallas kernels for 0% -> 0%
where the time goes in v1:
time: 329 us; the launch traced here: 323 us
  local copies, waits for them, and re-layouts  129 us (39%)
  loops' own time  59.8 us (18%)
  blocking collectives  48.7 us (15%)
  matrix products  35.1 us (11%)
  starting transfers between devices  32.9 us (10%)
  waiting for transfers between devices  11 us (3%)
  other arithmetic  5.07 us (2%)
    another operation x1, loops' own time, strip_update(): acc_real, acc_imag = lax.fori_loop(0, number, place, (zeros, zeros))  58.7 us
    gather x84, local copies, waits for them, and re-layouts  57.7 us
    unnamed x1, blocking collectives  42.9 us
    ppermute x12, starting transfers between devices, from_behind(): return lax.ppermute(shard, axis, pairs)  28 us
    dynamic_update_slice x14, local copies, waits for them, and re-layouts, place(): lax.dynamic_update_slice(acc_imag, window(acc_imag, top, left) + corr_ima...  23.8 us
    dynamic_update_slice x14, local copies, waits for them, and re-layouts, place(): lax.dynamic_update_slice(acc_real, window(acc_real, top, left) + corr_rea...  23.8 us
    dot_general x8, matrix products, left_apply(): return jnp.einsum('jk,bkl->bjl', table, batch, precision=highest)  15.7 us
    dot_general x8, matrix products, right_apply(): return jnp.einsum('bjk,kl->bjl', batch, table, precision=highest)  15.3 us
  transfers between devices with their start and end apart: 14, of which 4 were waited for; matrix products, arithmetic and copies ran while one was open for 2% of the time, Pallas kernels for 0%

profile of v1, /device:TPU:0, one launch (start us, length us, event | category | flops | bytes accessed | tf_op | source)
XLA Modules:
  0.0 323.0 jit_solution(7780633905037322923)
XLA Ops:
  3.4 11.1 %while.32 = (s32[]{:T(128)}, f32[32,896]{1,0:T(8,128)S(1)}, s32[]{:T(128)}, f32[2,2]{1,0:T(2,128)S(1)}, f32[2,32,896]{2,1,0:T(8,128)S(1)}, /*index=5*/s32[]{:T(128)}, s32[]{:T(128)}, s32[]{:T(128)}, f32[]{:T(128)}, f32[]{:T(128)}) while((s32[]{:T(128)}, f32[32,896]{1,0:T(8,128)S(1)}, s32[]{:T(128)}, f32[2,2]{1,0:T(2,128)S(1)}, ...), condition=%wide.region_1.2_spmd, body=%wide.region_0.1_spmd.sunk | while | flops 716821 | bytes 1147718 | solution.py:126
  3.4 3.0 collective-permute-start
  7.4 2.2 collective-permute-done
  9.6 1.8 collective-permute-start
  12.4 2.1 collective-permute-done
  14.5 3.7 %collective-permute-start.1 = (f32[32,896]{1,0:T(8,128)S(1)}, f32[32,896]{1,0:T(8,128)S(1)}, u32[]{:S(2)}, u32[]{:S(2)}) collective-permute-start(f32[32,896]{1,0:T(8,128)S(1)} %get-tuple-element.260), channel_id=1, source_target_pairs={{0,2},{1,3},{2,4},{3,5},{4,6},{5,7},{6,8},{7,9},{8,10},{9,11},{10,... | collective-permute-start | bytes 344072 | tf_op jit(solution)/shard_map/ppermute | solution.py:23
  24.9 5.7 %collective-permute-done.4 = f32[32,896]{1,0:T(8,128)S(1)} collective-permute-done((f32[32,896]{1,0:T(8,128)S(1)}, f32[32,896]{1,0:T(8,128)S(1)}, u32[]{:S(2)}, u32[]{:S(2)}) %collective-permute-start.4) | collective-permute-done | bytes 114720 | tf_op jit(solution)/shard_map/ppermute | solution.py:23
  31.4 29.6 %while.34 = (s32[]{:T(128)}, f32[160,1024]{1,0:T(8,128)S(1)}, s32[14,2]{0,1:T(2,128)S(1)}, f32[14,128,128]{2,1,0:T(8,128)S(1)}, s32[]{:T(128)}) while((s32[]{:T(128)}, f32[160,1024]{1,0:T(8,128)S(1)}, s32[14,2]{0,1:T(2,128)S(1)}, f32[14,128,128]{2,1,0:T(8,128)S(1)}, s32[]{:T(128)}) %tuple.120), condition=%wide.while_cond, body=%wide.while_body.sunk | while | flops 2 | bytes 131181 | solution.py:67
  61.3 29.1 %while.35 = (s32[]{:T(128)}, f32[160,1024]{1,0:T(8,128)S(1)}, s32[14,2]{0,1:T(2,128)S(1)}, f32[14,128,128]{2,1,0:T(8,128)S(1)}, s32[]{:T(128)}) while((s32[]{:T(128)}, f32[160,1024]{1,0:T(8,128)S(1)}, s32[14,2]{0,1:T(2,128)S(1)}, f32[14,128,128]{2,1,0:T(8,128)S(1)}, s32[]{:T(128)}) %tuple.127), condition=%wide.while_cond.1, body=%wide.while_body.1.sunk | while | flops 2 | bytes 131181 | solution.py:67
  90.7 1.7 fusion.42
  92.5 1.7 fusion.46
  94.2 1.8 fusion.10
  96.0 1.7 fusion.44
  97.7 1.7 fusion.31
  99.4 1.8 fusion.9
  101.2 1.9 convolution_subtract_fusion.2
  103.2 2.6 fusion.13
  105.7 2.2 fusion.14
  107.9 2.2 fusion.18
  110.1 2.2 fusion.8
  112.3 1.8 fusion.26
  114.1 1.9 fusion.38
  116.0 2.2 fusion.7
  118.2 1.8 fusion.5
  120.0 1.9 multiply_subtract_fusion
  122.0 126.6 %while.33 = (s32[]{:T(128)}, f32[160,1024]{1,0:T(8,128)S(1)}, f32[160,1024]{1,0:T(8,128)S(1)}, s32[14]{0:T(128)S(1)}, s32[14]{0:T(128)S(1)}, /*index=5*/f32[14,1...) while((s32[]{:T(128)}, f32[160,1024]{1,0:T(8,128)S(1)}, ...), condition=%wide.region_3.4_spmd, body=%wide.region_2.3_spmd.sunk | while | flops 32776 | bytes 655581 | solution.py:101
  127.7 1.7 dynamic_update_slice.17
  129.4 1.7 dynamic_update_slice.16
  136.7 1.7 dynamic_update_slice.17
  138.4 1.7 dynamic_update_slice.16
  154.8 1.7 dynamic_update_slice.17
  156.5 1.7 dynamic_update_slice.16
  190.9 1.7 dynamic_update_slice.17
  192.6 1.7 dynamic_update_slice.16
  200.0 1.7 dynamic_update_slice.17
  201.7 1.7 dynamic_update_slice.16
  209.1 1.7 dynamic_update_slice.17
  210.8 1.7 dynamic_update_slice.16
  218.1 1.7 dynamic_update_slice.17
  219.8 1.7 dynamic_update_slice.16
  245.2 1.7 dynamic_update_slice.17
  246.9 1.7 dynamic_update_slice.16
  250.2 3.0 collective-permute-start.11
  253.2 4.5 %collective-permute-start.12 = (f32[32,896]{1,0:T(8,128)S(1)}, f32[32,896]{1,0:T(8,128)S(1)}, u32[]{:S(2)}, u32[]{:S(2)}) collective-permute-start(f32[32,896]{1,0:T(8,128)S(1)} %get-tuple-element.348), channel_id=1, source_target_pairs={{0,2},{1,3},{2,4},{3,5},{4,6},{5,7},{6,8},{7,9},{8,10},{9,11},{10,... | collective-permute-start | bytes 344072 | tf_op jit(solution)/shard_map/ppermute | solution.py:23
  260.6 3.5 %collective-permute-start.7 = (f32[32,896]{1,0:T(8,128)S(1)}, f32[32,896]{1,0:T(8,128)S(1)}, u32[]{:S(2)}, u32[]{:S(2)}) collective-permute-start(f32[32,896]{1,0:T(8,128)S(1)} %get-tuple-element.345), channel_id=1, source_target_pairs={{0,1},{1,2},{2,3},{3,4},{4,5},{5,6},{6,7},{7,8},{8,9},{9,10},{10,1... | collective-permute-start | bytes 344072 | tf_op jit(solution)/shard_map/ppermute | solution.py:23
  264.0 4.3 %collective-permute-start.8 = (f32[32,896]{1,0:T(8,128)S(1)}, f32[32,896]{1,0:T(8,128)S(1)}, u32[]{:S(2)}, u32[]{:S(2)}) collective-permute-start(f32[32,896]{1,0:T(8,128)S(1)} %get-tuple-element.344), channel_id=1, source_target_pairs={{0,2},{1,3},{2,4},{3,5},{4,6},{5,7},{6,8},{7,9},{8,10},{9,11},{10,... | collective-permute-start | bytes 344072 | tf_op jit(solution)/shard_map/ppermute | solution.py:23
  270.4 42.9 %all-reduce.2 = f32[32]{0:T(128)S(1)} all-reduce(f32[32]{0:T(128)S(1)} %dynamic-update-slice.4), channel_id=1, replica_groups=mesh['blk'=2,'wide'=16] {'blk','wide'}, use_global_device_ids=true, to_apply=%add.2 | all-reduce | flops 32 | bytes 256
  314.4 5.8 %all-gather = f32[64,896]{1,0:T(8,128)S(1)} all-gather(f32[32,896]{1,0:T(8,128)S(1)} %multiply_subtract_fusion.2), channel_id=2, replica_groups=mesh['blk'=2,'wide'=16] {'blk'}, dimensions={0}, use_global_device_ids=true | all-gather | bytes 344064 | tf_op jit(solution)/shard_map/all_gather | solution.py:178
  (204 shorter events, 120.9 us)
Async XLA Ops:
  0.6 1.2 copy-start
  1.8 0.7 copy-start.1
  3.4 18.8 %copy-start.4 = (f32[2,128,128]{2,1,0:T(8,128)S(1)}, f32[2,128,128]{2,1,0:T(8,128)}, u32[]{:S(2)}) copy-start(f32[2,128,128]{2,1,0:T(8,128)} %param.12) | copy-start | bytes 393220
  3.4 6.2 %collective-permute-start = (f32[32,896]{1,0:T(8,128)S(1)}, f32[32,896]{1,0:T(8,128)S(1)}, u32[]{:S(2)}, u32[]{:S(2)}) collective-permute-start(f32[32,896]{1,0:T(8,128)S(1)} %get-tuple-element.514), channel_id=1, source_target_pairs={{0,16},{16,0},{1,17},{17,1},{2,18},{18,2},{3,19},{19,3},{4,20},{20... | collective-permute-start | bytes 344072 | tf_op jit(solution)/shard_map/while/body/eval_jaxpr/ppermute | solution.py:17
  9.6 4.9 %collective-permute-start = (f32[32,896]{1,0:T(8,128)S(1)}, f32[32,896]{1,0:T(8,128)S(1)}, u32[]{:S(2)}, u32[]{:S(2)}) collective-permute-start(f32[32,896]{1,0:T(8,128)S(1)} %get-tuple-element.514), channel_id=1, source_target_pairs={{0,16},{16,0},{1,17},{17,1},{2,18},{18,2},{3,19},{19,3},{4,20},{20... | collective-permute-start | bytes 344072 | tf_op jit(solution)/shard_map/while/body/eval_jaxpr/ppermute | solution.py:17
  14.5 7.6 %copy-start.5 = (s32[2,1,1,14]{3,2,1,0:T(1,128)S(1)}, s32[2,1,1,14]{3,2,1,0:T(1,128)}, u32[]{:S(2)}) copy-start(s32[2,1,1,14]{3,2,1,0:T(1,128)} %param.14) | copy-start | bytes 340
  14.5 7.7 %collective-permute-start.1 = (f32[32,896]{1,0:T(8,128)S(1)}, f32[32,896]{1,0:T(8,128)S(1)}, u32[]{:S(2)}, u32[]{:S(2)}) collective-permute-start(f32[32,896]{1,0:T(8,128)S(1)} %get-tuple-element.260), channel_id=1, source_target_pairs={{0,2},{1,3},{2,4},{3,5},{4,6},{5,7},{6,8},{7,9},{8,10},{9,11},{10,... | collective-permute-start | bytes 344072 | tf_op jit(solution)/shard_map/ppermute | solution.py:23
  18.2 4.5 %collective-permute-start.2 = (f32[32,896]{1,0:T(8,128)S(1)}, f32[32,896]{1,0:T(8,128)S(1)}, u32[]{:S(2)}, u32[]{:S(2)}) collective-permute-start(f32[32,896]{1,0:T(8,128)S(1)} %get-tuple-element.260), channel_id=1, source_target_pairs={{0,1},{1,2},{2,3},{3,4},{4,5},{5,6},{6,7},{7,8},{8,9},{9,10},{10,1... | collective-permute-start | bytes 344072 | tf_op jit(solution)/shard_map/ppermute | solution.py:23
  19.5 5.0 %collective-permute-start.3 = (f32[32,896]{1,0:T(8,128)S(1)}, f32[32,896]{1,0:T(8,128)S(1)}, u32[]{:S(2)}, u32[]{:S(2)}) collective-permute-start(f32[32,896]{1,0:T(8,128)S(1)} %get-tuple-element.260), channel_id=1, source_target_pairs={{1,0},{2,1},{3,2},{4,3},{5,4},{6,5},{7,6},{8,7},{9,8},{10,9},{11,1... | collective-permute-start | bytes 344072 | tf_op jit(solution)/shard_map/ppermute | solution.py:23
  20.8 9.8 %collective-permute-start.4 = (f32[32,896]{1,0:T(8,128)S(1)}, f32[32,896]{1,0:T(8,128)S(1)}, u32[]{:S(2)}, u32[]{:S(2)}) collective-permute-start(f32[32,896]{1,0:T(8,128)S(1)} %get-tuple-element.260), channel_id=1, source_target_pairs={{2,0},{3,1},{4,2},{5,3},{6,4},{7,5},{8,6},{9,7},{10,8},{11,9},{12,... | collective-permute-start | bytes 344072 | tf_op jit(solution)/shard_map/ppermute | solution.py:23
  101.2 1.9 copy-start.3
  248.9 11.7 %collective-permute-start.10 = (f32[32,896]{1,0:T(8,128)S(1)}, f32[32,896]{1,0:T(8,128)S(1)}, u32[]{:S(2)}, u32[]{:S(2)}) collective-permute-start(f32[32,896]{1,0:T(8,128)S(1)} %get-tuple-element.350), channel_id=1, source_target_pairs={{1,0},{2,1},{3,2},{4,3},{5,4},{6,5},{7,6},{8,7},{9,8},{10,9},{11,1... | collective-permute-start | bytes 344072 | tf_op jit(solution)/shard_map/ppermute | solution.py:23
  250.2 13.9 %collective-permute-start.11 = (f32[32,896]{1,0:T(8,128)S(1)}, f32[32,896]{1,0:T(8,128)S(1)}, u32[]{:S(2)}, u32[]{:S(2)}) collective-permute-start(f32[32,896]{1,0:T(8,128)S(1)} %get-tuple-element.349), channel_id=1, source_target_pairs={{0,1},{1,2},{2,3},{3,4},{4,5},{5,6},{6,7},{7,8},{8,9},{9,10},{10,1... | collective-permute-start | bytes 344072 | tf_op jit(solution)/shard_map/ppermute | solution.py:23
  253.2 15.1 %collective-permute-start.12 = (f32[32,896]{1,0:T(8,128)S(1)}, f32[32,896]{1,0:T(8,128)S(1)}, u32[]{:S(2)}, u32[]{:S(2)}) collective-permute-start(f32[32,896]{1,0:T(8,128)S(1)} %get-tuple-element.348), channel_id=1, source_target_pairs={{0,2},{1,3},{2,4},{3,5},{4,6},{5,7},{6,8},{7,9},{8,10},{9,11},{10,... | collective-permute-start | bytes 344072 | tf_op jit(solution)/shard_map/ppermute | solution.py:23
  257.9 55.9 %collective-permute-start.5 = (f32[32,896]{1,0:T(8,128)S(1)}, f32[32,896]{1,0:T(8,128)S(1)}, u32[]{:S(2)}, u32[]{:S(2)}) collective-permute-start(f32[32,896]{1,0:T(8,128)S(1)} %get-tuple-element.343), channel_id=1, source_target_pairs={{2,0},{3,1},{4,2},{5,3},{6,4},{7,5},{8,6},{9,7},{10,8},{11,9},{12,... | collective-permute-start | bytes 344072 | tf_op jit(solution)/shard_map/ppermute | solution.py:23
  259.2 54.6 %collective-permute-start.6 = (f32[32,896]{1,0:T(8,128)S(1)}, f32[32,896]{1,0:T(8,128)S(1)}, u32[]{:S(2)}, u32[]{:S(2)}) collective-permute-start(f32[32,896]{1,0:T(8,128)S(1)} %get-tuple-element.346), channel_id=1, source_target_pairs={{1,0},{2,1},{3,2},{4,3},{5,4},{6,5},{7,6},{8,7},{9,8},{10,9},{11,1... | collective-permute-start | bytes 344072 | tf_op jit(solution)/shard_map/ppermute | solution.py:23
  260.6 53.3 %collective-permute-start.7 = (f32[32,896]{1,0:T(8,128)S(1)}, f32[32,896]{1,0:T(8,128)S(1)}, u32[]{:S(2)}, u32[]{:S(2)}) collective-permute-start(f32[32,896]{1,0:T(8,128)S(1)} %get-tuple-element.345), channel_id=1, source_target_pairs={{0,1},{1,2},{2,3},{3,4},{4,5},{5,6},{6,7},{7,8},{8,9},{9,10},{10,1... | collective-permute-start | bytes 344072 | tf_op jit(solution)/shard_map/ppermute | solution.py:23
  264.0 49.8 %collective-permute-start.8 = (f32[32,896]{1,0:T(8,128)S(1)}, f32[32,896]{1,0:T(8,128)S(1)}, u32[]{:S(2)}, u32[]{:S(2)}) collective-permute-start(f32[32,896]{1,0:T(8,128)S(1)} %get-tuple-element.344), channel_id=1, source_target_pairs={{0,2},{1,3},{2,4},{3,5},{4,6},{5,7},{6,8},{7,9},{8,10},{9,11},{10,... | collective-permute-start | bytes 344072 | tf_op jit(solution)/shard_map/ppermute | solution.py:23
  268.3 45.5 %collective-permute-start.9 = (f32[32,896]{1,0:T(8,128)S(1)}, f32[32,896]{1,0:T(8,128)S(1)}, u32[]{:S(2)}, u32[]{:S(2)}) collective-permute-start(f32[32,896]{1,0:T(8,128)S(1)} %get-tuple-element.347), channel_id=1, source_target_pairs={{2,0},{3,1},{4,2},{5,3},{6,4},{7,5},{8,6},{9,7},{10,8},{11,9},{12,... | collective-permute-start | bytes 344072 | tf_op jit(solution)/shard_map/ppermute | solution.py:23
  314.3 5.9 %copy-start.2 = (f32[1,2,32,896]{3,1,2,0:T(2,128)S(1)}, f32[1,2,32,896]{3,1,2,0:T(2,128)}, u32[]{:S(2)}) copy-start(f32[1,2,32,896]{3,1,2,0:T(2,128)} %copy-done.1) | copy-start | bytes 688132
  320.2 0.7 copy-start.6
